TPU v7x, 32 devices: a whole 2x2x4 slice. The times are simulated.
32 devices in a mesh: ctx: 4 (over z), tp: 4 (over y, core), ep: 2 (over x).
Axes of the slice: x: 2, y: 2, z: 4, core: 2. Of those that a mesh axis runs over, the one named last changes fastest.
Arguments:
- resid: bfloat16 [1024, 6144], P('ctx', ('tp', 'ep')), may hold values from -60 to 60
- queries: bfloat16 [1024, 6144], P('ctx', 'tp'), may hold values from -6 to 6
- keys: bfloat16 [1024, 1024], P('ctx', 'tp'), may hold values from -4 to 4
- values: bfloat16 [1024, 1024], P('ctx', 'tp'), may hold values from -5 to 5
- w_out: bfloat16 [6144, 6144], P('tp', ('ctx', 'ep')), may hold values from -0.078125 to 0.078125
- norm_gain: bfloat16 [6144], P(('tp', 'ep')), may hold values from 0.5 to 1.5
- w_gate: bfloat16 [4, 6144, 8192], P('tp', None, ('ctx', 'ep')), may hold values from -0.078125 to 0.078125
- w_up: bfloat16 [4, 6144, 8192], P('tp', None, ('ctx', 'ep')), may hold values from -0.078125 to 0.078125
- w_down: bfloat16 [4, 8192, 6144], P('tp', ('ctx', 'ep')), may hold values from -0.0625 to 0.0625
- expert_ids: int32 [1024, 2], P('ctx'), may hold values from 0 to 3, all different within a row; in each aligned block of 256 rows (0 to 255, 256 to 511, ...) at most 192 rows name the same one
- route_units: int32 [1024, 2], P('ctx'), may hold values from 1 to 65535
Outputs:
- mixed: bfloat16 [1024, 6144], P('ctx', ('tp', 'ep'))
Inputs may be any that keep to these rules, and one draw needn't show every extreme that they name: `expert_ids`: each row names two different experts; in every aligned block of 256 rows no expert is named by more than 192 rows, a bound that some block reaches.
All inputs are finite; a program needn't handle non-finite values.
Results may differ from a plain program's by a relative error of at most 0.01.
Values may be sent and summed in bfloat16 or wider, within the bound.
A program may use at most 128 MiB of HBM per device.

v0:
```python
import jax
import jax.numpy as jnp
from jax import lax
from jax.sharding import PartitionSpec as P

D = 6144
HD = 128


def from_partner(x, axis, distance):
    return lax.ppermute(x, axis, [(i, i ^ 1 << distance) for i in range(lax.axis_size(axis))])


def on_device(
    resid, queries, keys, values, w_out, norm_gain, w_gate, w_up, w_down, expert_ids, route_units
):
    tp_size = lax.axis_size("tp")
    ep_size = lax.axis_size("ep")
    ctx_size = lax.axis_size("ctx")
    tok_rows = queries.shape[0]
    heads_dev = queries.shape[1] // HD
    kv_dev = keys.shape[1] // HD
    group = heads_dev // kv_dev
    feat_dev = resid.shape[1]
    hidden_dev = w_gate.shape[2]
    capacity = 3 * tok_rows // tp_size
    first_pos = lax.axis_index("ctx") * tok_rows
    query_heads = queries.reshape(tok_rows, kv_dev, group, HD)
    query_pos = first_pos + jnp.arange(tok_rows, dtype=jnp.int32)
    running_max = jnp.full((kv_dev, group, tok_rows), -1e30, jnp.float32)
    key_piece = lax.all_gather(keys, "ctx", axis=0, tiled=True)
    value_piece = lax.all_gather(values, "ctx", axis=0, tiled=True)
    count = key_piece.shape[0]
    key_rows = key_piece.reshape(count, kv_dev, HD)
    value_rows = value_piece.reshape(count, kv_dev, HD)
    scores = jnp.einsum(
        "tkgd,nkd->kgtn", query_heads, key_rows, preferred_element_type=jnp.float32
    ) * HD ** (-0.5)
    key_pos = jnp.arange(count, dtype=jnp.int32)
    allowed = (key_pos[None, :] <= query_pos[:, None])[None, None]
    block_max = jnp.max(jnp.where(allowed, scores, -1e30), axis=-1)
    new_max = jnp.maximum(running_max, block_max)
    probs = jnp.where(allowed, jnp.exp(scores - new_max[..., None]), 0.0)
    new_sum = jnp.sum(probs, axis=-1)
    probs_b = probs.astype(jnp.bfloat16)
    update = jnp.einsum("kgtn,nkd->kgtd", probs_b, value_rows, preferred_element_type=jnp.float32)
    attn = (
        (update / new_sum[..., None])
        .transpose(2, 0, 1, 3)
        .reshape(tok_rows, heads_dev * HD)
        .astype(jnp.bfloat16)
    )
    partial_proj = jnp.dot(
        attn, lax.all_gather(w_out, "ctx", axis=1, tiled=True), preferred_element_type=jnp.float32
    )
    proj = lax.psum_scatter(
        partial_proj.astype(jnp.bfloat16), "tp", scatter_dimension=1, tiled=True
    ).astype(jnp.float32)
    hres = (resid.astype(jnp.float32) + proj).astype(jnp.bfloat16)
    hfloat = hres.astype(jnp.float32)
    square_total = lax.psum(jnp.sum(hfloat * hfloat, axis=1, keepdims=True), ("tp", "ep"))
    normed = (hfloat * lax.rsqrt(square_total / D + 1e-05) * norm_gain.astype(jnp.float32)).astype(
        jnp.bfloat16
    )
    onehot = (expert_ids[..., None] == jnp.arange(tp_size, dtype=jnp.int32)).astype(jnp.int32)
    per_token = jnp.sum(onehot, axis=1)
    earlier = jnp.cumsum(per_token, axis=0) - per_token
    slot = jnp.sum(onehot * earlier[:, None, :], axis=-1)
    codes = expert_ids * capacity + slot
    slot_ids = jnp.arange(tp_size * capacity, dtype=jnp.int32)
    picks = (
        (slot_ids[:, None] == codes[None, :, 0]) | (slot_ids[:, None] == codes[None, :, 1])
    ).astype(jnp.bfloat16)
    dispatched = jnp.dot(picks, normed, preferred_element_type=jnp.float32).astype(jnp.bfloat16)
    dispatched = dispatched.reshape(tp_size, 1, capacity, feat_dev)
    arrived = lax.all_to_all(dispatched, "tp", split_axis=0, concat_axis=1, tiled=True)
    gate_w = w_gate[0].reshape(tp_size, ep_size, feat_dev, hidden_dev)
    up_w = w_up[0].reshape(tp_size, ep_size, feat_dev, hidden_dev)
    zero_acc = jnp.zeros((ctx_size, capacity, hidden_dev), jnp.float32)
    piece = lax.all_gather(arrived, ("ctx", "ep"), axis=0, tiled=True)

    def one_row(index, totals):
        gate_total, up_total = totals
        source = index // ep_size
        parity = index % ep_size
        row = lax.dynamic_index_in_dim(piece, index, 0, keepdims=False)
        gate_part = lax.dynamic_index_in_dim(gate_w, parity, 1, keepdims=False)
        up_part = lax.dynamic_index_in_dim(up_w, parity, 1, keepdims=False)
        gate_add = jnp.einsum("tsj,tjf->sf", row, gate_part, preferred_element_type=jnp.float32)
        up_add = jnp.einsum("tsj,tjf->sf", row, up_part, preferred_element_type=jnp.float32)
        gate_now = lax.dynamic_index_in_dim(gate_total, source, 0, keepdims=False) + gate_add
        up_now = lax.dynamic_index_in_dim(up_total, source, 0, keepdims=False) + up_add
        return (
            lax.dynamic_update_index_in_dim(gate_total, gate_now, source, 0),
            lax.dynamic_update_index_in_dim(up_total, up_now, source, 0),
        )

    gate_acc, up_acc = lax.fori_loop(0, piece.shape[0], one_row, (zero_acc, zero_acc))
    hidden = (jax.nn.silu(gate_acc) * up_acc).astype(jnp.bfloat16)
    down_w = w_down[0].reshape(hidden_dev, tp_size, ep_size, feat_dev)
    parity = lax.axis_index("ep")
    mine_cols = lax.dynamic_index_in_dim(down_w, parity, 2, keepdims=False)
    give_cols = lax.dynamic_index_in_dim(down_w, 1 - parity, 2, keepdims=False)
    got_hidden, got_cols = from_partner((hidden, give_cols), "ep", 0)
    hidden_both = jnp.concatenate([hidden, got_hidden], axis=2)
    cols_both = jnp.concatenate([mine_cols, got_cols], axis=0)
    blocks = lax.axis_size("ctx") * capacity // capacity
    product = jnp.einsum(
        "csf,ftj->cstj", hidden_both, cols_both, preferred_element_type=jnp.float32
    )
    expert_sum = lax.psum_scatter(
        product.reshape(blocks * capacity, tp_size * feat_dev).astype(jnp.bfloat16),
        "ctx",
        scatter_dimension=0,
        tiled=True,
    )
    expert_out = expert_sum.reshape(1, capacity, tp_size, feat_dev)
    returned = lax.all_to_all(expert_out, "tp", split_axis=2, concat_axis=0, tiled=True)
    units = route_units.astype(jnp.float32)
    weights = (units / jnp.sum(units, axis=-1, keepdims=True)).astype(jnp.bfloat16)
    combine = jnp.where(slot_ids[None, :] == codes[:, 0:1], weights[:, 0:1], 0.0) + jnp.where(
        slot_ids[None, :] == codes[:, 1:2], weights[:, 1:2], 0.0
    )
    moe = jnp.dot(
        combine, returned.reshape(tp_size * capacity, feat_dev), preferred_element_type=jnp.float32
    )
    return (hfloat + moe).astype(jnp.bfloat16)


def solution(mesh):
    placed = (
        P("ctx", ("tp", "ep")),
        P("ctx", "tp"),
        P("ctx", "tp"),
        P("ctx", "tp"),
        P("tp", ("ctx", "ep")),
        P(("tp", "ep")),
        P("tp", None, ("ctx", "ep")),
        P("tp", None, ("ctx", "ep")),
        P("tp", ("ctx", "ep"), None),
        P("ctx", None),
        P("ctx", None),
    )
    return jax.shard_map(
        on_device, mesh=mesh, in_specs=placed, out_specs=P("ctx", ("tp", "ep")), check_vma=False
    )
```

profile of v0, /device:TPU:0, one launch (start us, length us, event | category | flops | bytes accessed | tf_op | source)
XLA Modules:
  0.0 699.3 jit_solution(8056801487796941439)
XLA Ops:
  7.3 19.0 %all_gather.13 = bf16[1024,256]{1,0:T(8,128)(2,1)S(1)} all-gather(bf16[256,256]{1,0:T(8,128)(2,1)} %param.16), channel_id=1, replica_groups=mesh['ctx'=4,'tp'=4,'ep'=2] {'ctx'}, dimensions={0}, use_global_device_ids=true | all-gather | bytes 655360 | tf_op jit(solution)/shard_map/all_gather | solution.py:32
  28.9 24.0 %all_gather.12 = bf16[1024,256]{0,1:T(8,128)(2,1)S(1)} all-gather(bf16[256,256]{0,1:T(8,128)(2,1)S(1)} %copy.54), channel_id=1, replica_groups=mesh['ctx'=4,'tp'=4,'ep'=2] {'ctx'}, dimensions={0}, use_global_device_ids=true | all-gather | bytes 655360 | tf_op jit(solution)/shard_map/all_gather | solution.py:31
  60.5 126.2 %all-gather.4.cloned.1.call-done = bf16[1536,3072]{1,0:T(8,128)(2,1)} async-done(((bf16[1536,768]{1,0:T(8,128)(2,1)}), bf16[1536,3072]{1,0:T(8,128)(2,1)}) %all-gather.4.cloned.1.call-update) | async-done | bytes 9437200 | tf_op jit(solution)/shard_map/all_gather | solution.py:54
  186.8 7.5 %convolution_convert_fusion = bf16[256,3072]{1,0:T(8,128)(2,1)} fusion(bf16[256,1536]{0,1:T(8,128)(2,1)S(1)} %bitcast.174, bf16[1536,3072]{1,0:T(8,128)(2,1)} %all-gather.4.cloned.1.call-done), kind=kOutput, calls=%fused_computation.37 | convolution fusion | flops 2416705536 | bytes 11796480 | tf_op jit(solution)/shard_map/dot_general | solution.py:53
  196.1 25.5 %reduce-scatter.3.cloned.1.call-done = bf16[256,768]{1,0:T(8,128)(2,1)} async-done(((bf16[256,3072]{1,0:T(8,128)(2,1)}), bf16[256,768]{1,0:T(8,128)(2,1)}) %reduce-scatter.3.cloned.1.call-update) | async-done | bytes 393232 | tf_op jit(solution)/shard_map/reduce_scatter | solution.py:56
  222.8 13.3 %psum.7 = f32[256,1]{0,1:T(1,128)S(1)} all-reduce(f32[256,1]{0,1:T(1,128)S(1)} %bitcast.180), channel_id=1, replica_groups=mesh['ctx'=4,'tp'=4,'ep'=2] {'tp','ep'}, use_global_device_ids=true, to_apply=%region_9.10 | all-reduce | flops 256 | bytes 2048 | tf_op jit(solution)/shard_map/psum | solution.py:61
  237.7 19.0 %all_to_all.27 = bf16[4,1,192,768]{3,2,1,0:T(8,128)(2,1)} all-to-all(bf16[4,1,192,768]{3,2,1,0:T(8,128)(2,1)S(1)} %bitcast.176), channel_id=1, replica_groups=mesh['ctx'=4,'tp'=4,'ep'=2] {'tp'}, dimensions={0} | all-to-all | bytes 2359296 | tf_op jit(solution)/shard_map/all_to_all | solution.py:76
  257.0 27.5 %reshape_squeeze.11 = bf16[1024,4,2,768]{3,2,1,0:T(2,128)(2,1)} reshape(bf16[1,1024,6144]{2,1,0:T(8,128)(2,1)} %param.21) | data formatting | bytes 25165824 | tf_op jit(solution)/shard_map/reshape;squeeze | solution.py:100
  284.4 29.1 %constant_dynamic-slice_fusion.2 = (bf16[1024,4,1,768]{3,2,1,0:T(2,128)(2,1)}, bf16[1024,4,1,768]{3,2,1,0:T(2,128)(2,1)}) fusion(bf16[1024,4,2,768]{3,2,1,0:T(2,128)(2,1)} %reshape_squeeze.11, s32[]{:T(128)S(6)} %select_n.93, s32[]{:T(128)S(6)} %select_n.94), kind=kLoop, calls=%fused_computation.87 | loop fusion | bytes 25165832 | tf_op jit(solution)/shard_map/jit(dynamic_index_in_dim)/dynamic_slice | solution.py:102
  313.5 9.5 %copy.85 = bf16[1024,4,1,768]{3,0,1,2:T(8,128)(2,1)} copy(bf16[1024,4,1,768]{3,2,1,0:T(2,128)(2,1)} %get-tuple-element.200) | data formatting | bytes 12582912
  324.1 106.9 %all-gather.6.cloned.1.call-done = bf16[32,1,192,768]{3,2,1,0:T(8,128)(2,1)} async-done(((bf16[4,1,192,768]{3,2,1,0:T(8,128)(2,1)}), bf16[32,1,192,768]{3,2,1,0:T(8,128)(2,1)}) %all-gather.6.cloned.1.call-update) | async-done | bytes 9437200 | tf_op jit(solution)/shard_map/all_gather | solution.py:80
  433.5 90.3 %while.17 = (s32[]{:T(128)}, f32[4,192,1024]{2,1,0:T(8,128)S(1)}, f32[4,192,1024]{2,1,0:T(8,128)}, bf16[8,4,192,768]{3,2,1,0:T(8,128)(2,1)}, bf16[4,2,768,1024]{...) while((s32[]{:T(128)}, f32[4,192,1024]{2,1,0:T(8,128)S(1)}, ...), condition=%wide.region_11.12_spmd, body=%wide.region_10.11_spmd.sunk | while | flops 2416312320 | bytes 21233992 | solution.py:98
  439.3 5.5 fusion.98
  450.7 5.5 fusion.98
  462.0 5.4 fusion.98
  473.2 5.4 fusion.98
  484.5 5.4 fusion.98
  507.1 5.5 fusion.98
  518.3 5.5 fusion.98
  527.8 6.7 copy.86
  534.6 28.3 %collective-permute-done = bf16[4,192,1024]{2,1,0:T(8,128)(2,1)} collective-permute-done((bf16[4,192,1024]{2,1,0:T(8,128)(2,1)}, bf16[4,192,1024]{2,1,0:T(8,128)(2,1)}, u32[]{:S(2)}, u32[]{:S(2)}) %collective-permute-start) | collective-permute-done | bytes 1572896 | tf_op jit(solution)/shard_map/ppermute | solution.py:11
  562.8 13.0 %fusion.49 = bf16[4,192,4,768]{3,1,2,0:T(8,128)(2,1)S(1)} fusion(bf16[1024,4,768]{2,0,1:T(8,128)(2,1)} %collective-permute-done.1, bf16[1024,4,768]{2,0,1:T(8,128)(2,1)S(1)} %bitcast.171, bf16[4,192,1024]{2,1,0:T(8,128)(2,1)} %collective-permute-done, bf16[4,192,1024]{2,1,0:T(8,128)(2,1)} %multiply_convert_fusion), kind=kOutput, calls=%fused_computation.42 | convolution fusion | flops 9697492992 | bytes 20447232 | tf_op jit(solution)/shard_map/csf,ftj->cstj/dot_general | solution.py:108
  582.7 85.5 %reduce-scatter.5.cloned.1.call-done = bf16[192,3072]{1,0:T(8,128)(2,1)} async-done(((bf16[768,3072]{1,0:T(8,128)(2,1)}), bf16[192,3072]{1,0:T(8,128)(2,1)}) %reduce-scatter.5.cloned.1.call-update) | async-done | bytes 1179664 | tf_op jit(solution)/shard_map/reduce_scatter | solution.py:111
  675.6 15.7 %all-to-all-done.1 = bf16[1,192,4,768]{3,1,0,2:T(8,128)(2,1)S(1)} async-done(((bf16[1,192,4,768]{3,1,0,2:T(8,128)(2,1)}), bf16[1,192,4,768]{3,1,0,2:T(8,128)(2,1)S(1)}, u32[]{:S(2)}, u32[]{:S(2)}) %all-to-all-start.1) | async-done | bytes 1179680 | tf_op jit(solution)/shard_map/all_to_all | solution.py:118
  (76 shorter events, 90.9 us)
Async XLA Ops:
  6.5 180.2 %all-gather.4.cloned.1.call-start = ((), (), s32[]{:S(2)}) async-start(), calls=%async_computation.4 | async-start | bytes 11796480 | tf_op jit(solution)/shard_map/all_gather | solution.py:54
  7.3 214.3 %reduce-scatter.3.cloned.1.call-start = ((), (), s32[]{:S(2)}) async-start(), calls=%async_computation.5 | async-start | bytes 1966080 | tf_op jit(solution)/shard_map/reduce_scatter | solution.py:56
  186.8 7.6 %copy-start.4 = (bf16[768]{0:T(1024)(128)(2,1)S(1)}, bf16[768]{0:T(1024)(128)(2,1)}, u32[]{:S(2)}) copy-start(bf16[768]{0:T(1024)(128)(2,1)} %param.18) | copy-start | bytes 4612
  186.8 7.6 %copy-start.2 = (s32[256,2]{0,1:T(2,128)S(1)}, s32[256,2]{0,1:T(2,128)}, u32[]{:S(2)}) copy-start(s32[256,2]{0,1:T(2,128)} %param.22) | copy-start | bytes 6148
  186.8 34.8 %copy-start = (bf16[256,768]{1,0:T(8,128)(2,1)S(1)}, bf16[256,768]{1,0:T(8,128)(2,1)}, u32[]{:S(2)}) copy-start(bf16[256,768]{1,0:T(8,128)(2,1)} %param.13) | copy-start | bytes 1179652
  194.3 236.7 %all-gather.6.cloned.1.call-start = ((), (), s32[]{:S(2)}) async-start(), calls=%async_computation.7 | async-start | bytes 10616832 | tf_op jit(solution)/shard_map/all_gather | solution.py:80
  256.8 411.4 %reduce-scatter.5.cloned.1.call-start = ((), (), s32[]{:S(2)}) async-start(), calls=%async_computation.6 | async-start | bytes 5898240 | tf_op jit(solution)/shard_map/reduce_scatter | solution.py:111
  323.1 211.5 %collective-permute-start.1 = (bf16[1024,4,768]{2,0,1:T(8,128)(2,1)}, bf16[1024,4,768]{2,0,1:T(8,128)(2,1)}, u32[]{:S(2)}, u32[]{:S(2)}) collective-permute-start(bf16[1024,4,768]{2,0,1:T(8,128)(2,1)} %bitcast.144), channel_id=1, source_target_pairs={{0,1},{1,0},{2,3},{3,2},{4,5},{5,4},{6,7},{7,6},{8,9},{9,8},{10,11... | collective-permute-start | bytes 18874376 | tf_op jit(solution)/shard_map/ppermute | solution.py:11
  527.8 35.0 %collective-permute-start = (bf16[4,192,1024]{2,1,0:T(8,128)(2,1)}, bf16[4,192,1024]{2,1,0:T(8,128)(2,1)}, u32[]{:S(2)}, u32[]{:S(2)}) collective-permute-start(bf16[4,192,1024]{2,1,0:T(8,128)(2,1)} %multiply_convert_fusion), channel_id=1, source_target_pairs={{0,1},{1,0},{2,3},{3,2},{4,5},{5,4},{6,7},{7,6},{8,9},{9,8},{10,11... | collective-permute-start | bytes 4718600 | tf_op jit(solution)/shard_map/ppermute | solution.py:11
  582.7 92.9 %copy-start.3 = (s32[256,2]{0,1:T(2,128)S(1)}, s32[256,2]{0,1:T(2,128)}, u32[]{:S(2)}) copy-start(s32[256,2]{0,1:T(2,128)} %param.23) | copy-start | bytes 6148
  582.7 108.7 %copy-start.1 = (bf16[256,768]{1,0:T(8,128)(2,1)S(1)}, bf16[256,768]{1,0:T(8,128)(2,1)}, u32[]{:S(2)}) copy-start(bf16[256,768]{1,0:T(8,128)(2,1)} %reduce-scatter.3.cloned.1.call-done) | copy-start | bytes 1179652
  672.0 19.3 %all-to-all-start.1 = ((bf16[1,192,4,768]{3,1,0,2:T(8,128)(2,1)}), bf16[1,192,4,768]{3,1,0,2:T(8,128)(2,1)S(1)}, u32[]{:S(2)}, u32[]{:S(2)}) async-start(bf16[1,192,4,768]{3,1,0,2:T(8,128)(2,1)} %copy.68), calls=%async_computation.3 | async-start | bytes 2359296 | tf_op jit(solution)/shard_map/all_to_all | solution.py:118
Sparse Core Ops, SparseCore 0:
  8.9 177.8 all-gather.3
  194.4 27.0 reduce-scatter.2
  256.9 174.1 all-gather.5
  582.8 85.2 reduce-scatter.4
where the time goes:
time: 701 us; the launch traced here: 699 us
  waiting for transfers between devices  389 us (55%)
  matrix products  108 us (15%)
  local copies, waits for them, and re-layouts  98.9 us (14%)
  blocking collectives  75.3 us (11%)
  between operations  13.3 us (2%)
  other arithmetic  9.34 us (1%)
    all_gather x1, waiting for transfers between devices, on_device(): lax.all_gather(w_out, 'ctx', axis=1, tiled=True)  126 us
    all_gather x1, waiting for transfers between devices, on_device(): piece = lax.all_gather(arrived, ('ctx', 'ep'), axis=0, tiled=True)  107 us
    reduce_scatter x1, waiting for transfers between devices, on_device(): lax.psum_scatter(product.reshape(blocks * capacity, tp_size * feat_dev).a...  85.5 us
    dot_general x8, matrix products, one_row(): jnp.einsum('tsj,tjf->sf', row, up_part, preferred_element_type=jnp.float32)  43.6 us
    dot_general x8, matrix products, one_row(): jnp.einsum('tsj,tjf->sf', row, gate_part, preferred_element_type=jnp.floa...  36.5 us
    dynamic_slice x1, local copies, waits for them, and re-layouts, on_device(): mine_cols = lax.dynamic_index_in_dim(down_w, parity, 2, keepdims=False)  29.1 us
    ppermute x2, waiting for transfers between devices, from_partner(): lax.ppermute(x, axis, [(i, i ^ 1 << distance) for i in range(lax.axis_siz...  28.3 us
    another operation x1, local copies, waits for them, and re-layouts, on_device(): down_w = w_down[0].reshape(hidden_dev, tp_size, ep_size, feat_dev)  27.5 us
  transfers between devices with their start and end apart: 7, of which 6 were waited for; matrix products, arithmetic and copies ran while one was open for 26% of the time, Pallas kernels for 0%

commit v1 on v0

--- a/solution.py
+++ b/solution.py
@@ -77,7 +77,12 @@
     gate_w = w_gate[0].reshape(tp_size, ep_size, feat_dev, hidden_dev)
     up_w = w_up[0].reshape(tp_size, ep_size, feat_dev, hidden_dev)
     zero_acc = jnp.zeros((ctx_size, capacity, hidden_dev), jnp.float32)
-    piece = lax.all_gather(arrived, ("ctx", "ep"), axis=0, tiled=True)
+    piece = jnp.concatenate(
+        lax.all_to_all(
+            jnp.stack([arrived for _ in range(lax.axis_size(("ctx", "ep")))]), ("ctx", "ep"), 0, 0
+        ),
+        axis=0,
+    )
 
     def one_row(index, totals):
         gate_total, up_total = totals

time: 701 us -> 741 us (1.057)
  waiting for transfers between devices: 389 us -> 418 us
    all_to_all x0 -> x1, waiting for transfers between devices: none -> 138 us  [on_device(): lax.all_to_all(jnp.stack([arrived for _ in range(lax.axis_size(('ctx', 'e...]
    all_gather x1 -> x0, waiting for transfers between devices: 107 us -> none  [on_device(): piece = lax.all_gather(arrived, ('ctx', 'ep'), axis=0, tiled=True)]
  transfers between devices with their start and end apart: 7 -> 7, of which waited for: 6 -> 6; matrix products, arithmetic and copies ran while one was open for 26% -> 24% of each run, Pallas kernels for 0% -> 0%
where the time goes in v1:
time: 741 us; the launch traced here: 739 us
  waiting for transfers between devices  418 us (56%)
  matrix products  108 us (15%)
  local copies, waits for them, and re-layouts  103 us (14%)
  blocking collectives  74.6 us (10%)
  between operations  13.3 us (2%)
  starting transfers between devices  12 us (2%)
  other arithmetic  9.34 us (1%)
    all_to_all x1, waiting for transfers between devices, on_device(): lax.all_to_all(jnp.stack([arrived for _ in range(lax.axis_size(('ctx', 'e...  138 us
    all_gather x1, waiting for transfers between devices, on_device(): lax.all_gather(w_out, 'ctx', axis=1, tiled=True)  126 us
    reduce_scatter x1, waiting for transfers between devices, on_device(): lax.psum_scatter(product.reshape(blocks * capacity, tp_size * feat_dev).a...  85 us
    dot_general x8, matrix products, one_row(): jnp.einsum('tsj,tjf->sf', row, up_part, preferred_element_type=jnp.float32)  43.6 us
    dot_general x8, matrix products, one_row(): jnp.einsum('tsj,tjf->sf', row, gate_part, preferred_element_type=jnp.floa...  36.5 us
    dynamic_slice x1, local copies, waits for them, and re-layouts, on_device(): mine_cols = lax.dynamic_index_in_dim(down_w, parity, 2, keepdims=False)  29.1 us
    another operation x1, local copies, waits for them, and re-layouts, on_device(): down_w = w_down[0].reshape(hidden_dev, tp_size, ep_size, feat_dev)  27.4 us
    ppermute x2, waiting for transfers between devices, from_partner(): lax.ppermute(x, axis, [(i, i ^ 1 << distance) for i in range(lax.axis_siz...  27.3 us
  transfers between devices with their start and end apart: 7, of which 6 were waited for; matrix products, arithmetic and copies ran while one was open for 24% of the time, Pallas kernels for 0%

profile of v1, /device:TPU:0, one launch (start us, length us, event | category | flops | bytes accessed | tf_op | source)
XLA Modules:
  0.0 739.3 jit_solution(14117879943570221539)
XLA Ops:
  7.3 19.0 %all_gather.10 = bf16[1024,256]{1,0:T(8,128)(2,1)S(1)} all-gather(bf16[256,256]{1,0:T(8,128)(2,1)} %param.16), channel_id=1, replica_groups=mesh['ctx'=4,'tp'=4,'ep'=2] {'ctx'}, dimensions={0}, use_global_device_ids=true | all-gather | bytes 655360 | tf_op jit(solution)/shard_map/all_gather | solution.py:32
  28.9 24.0 %all_gather.9 = bf16[1024,256]{0,1:T(8,128)(2,1)S(1)} all-gather(bf16[256,256]{0,1:T(8,128)(2,1)S(1)} %copy.54), channel_id=1, replica_groups=mesh['ctx'=4,'tp'=4,'ep'=2] {'ctx'}, dimensions={0}, use_global_device_ids=true | all-gather | bytes 655360 | tf_op jit(solution)/shard_map/all_gather | solution.py:31
  60.5 126.2 %all-gather.2.cloned.1.call-done = bf16[1536,3072]{1,0:T(8,128)(2,1)} async-done(((bf16[1536,768]{1,0:T(8,128)(2,1)}), bf16[1536,3072]{1,0:T(8,128)(2,1)}) %all-gather.2.cloned.1.call-update) | async-done | bytes 9437200 | tf_op jit(solution)/shard_map/all_gather | solution.py:54
  186.8 7.5 %convolution_convert_fusion = bf16[256,3072]{1,0:T(8,128)(2,1)} fusion(bf16[256,1536]{0,1:T(8,128)(2,1)S(1)} %bitcast.175, bf16[1536,3072]{1,0:T(8,128)(2,1)} %all-gather.2.cloned.1.call-done), kind=kOutput, calls=%fused_computation.37 | convolution fusion | flops 2416705536 | bytes 11796480 | tf_op jit(solution)/shard_map/dot_general | solution.py:53
  196.0 25.5 %reduce-scatter.3.cloned.1.call-done = bf16[256,768]{1,0:T(8,128)(2,1)} async-done(((bf16[256,3072]{1,0:T(8,128)(2,1)}), bf16[256,768]{1,0:T(8,128)(2,1)}) %reduce-scatter.3.cloned.1.call-update) | async-done | bytes 393232 | tf_op jit(solution)/shard_map/reduce_scatter | solution.py:56
  222.8 13.3 %psum.7 = f32[256,1]{0,1:T(1,128)S(1)} all-reduce(f32[256,1]{0,1:T(1,128)S(1)} %bitcast.181), channel_id=1, replica_groups=mesh['ctx'=4,'tp'=4,'ep'=2] {'tp','ep'}, use_global_device_ids=true, to_apply=%region_9.10 | all-reduce | flops 256 | bytes 2048 | tf_op jit(solution)/shard_map/psum | solution.py:61
  237.7 18.3 %all_to_all.29 = bf16[4,1,192,768]{3,2,1,0:T(8,128)(2,1)S(1)} all-to-all(bf16[4,1,192,768]{3,2,1,0:T(8,128)(2,1)S(1)} %bitcast.177), channel_id=1, replica_groups=mesh['ctx'=4,'tp'=4,'ep'=2] {'tp'}, dimensions={0} | all-to-all | bytes 2359296 | tf_op jit(solution)/shard_map/all_to_all | solution.py:76
  265.9 27.4 %reshape_squeeze.11 = bf16[1024,4,2,768]{3,2,1,0:T(2,128)(2,1)} reshape(bf16[1,1024,6144]{2,1,0:T(8,128)(2,1)} %param.21) | data formatting | bytes 25165824 | tf_op jit(solution)/shard_map/reshape;squeeze | solution.py:105
  293.2 29.1 %constant_dynamic-slice_fusion.2 = (bf16[1024,4,1,768]{3,2,1,0:T(2,128)(2,1)}, bf16[1024,4,1,768]{3,2,1,0:T(2,128)(2,1)}) fusion(bf16[1024,4,2,768]{3,2,1,0:T(2,128)(2,1)} %reshape_squeeze.11, s32[]{:T(128)S(6)} %select_n.93, s32[]{:T(128)S(6)} %select_n.94), kind=kLoop, calls=%fused_computation.87 | loop fusion | bytes 25165832 | tf_op jit(solution)/shard_map/jit(dynamic_index_in_dim)/dynamic_slice | solution.py:107
  322.3 9.4 %copy.85 = bf16[1024,4,1,768]{3,0,1,2:T(8,128)(2,1)} copy(bf16[1024,4,1,768]{3,2,1,0:T(2,128)(2,1)} %get-tuple-element.200) | data formatting | bytes 12582912
  333.4 137.7 %all-to-all-done.1 = bf16[8,1,4,192,768]{4,3,2,1,0:T(8,128)(2,1)} async-done(((bf16[8,1,4,192,768]{4,3,2,1,0:T(8,128)(2,1)}), bf16[8,1,4,192,768]{4,3,2,1,0:T(8,128)(2,1)}, u32[]{:S(2)}, u32[]{:S(2)}) %all-to-all-start.1) | async-done | bytes 9437216 | tf_op jit(solution)/shard_map/all_to_all | solution.py:81
  473.6 90.3 %while.17 = (s32[]{:T(128)}, f32[4,192,1024]{2,1,0:T(8,128)S(1)}, f32[4,192,1024]{2,1,0:T(8,128)}, bf16[8,4,192,768]{3,2,1,0:T(8,128)(2,1)}, bf16[4,2,768,1024]{...) while((s32[]{:T(128)}, f32[4,192,1024]{2,1,0:T(8,128)S(1)}, ...), condition=%wide.region_11.12_spmd, body=%wide.region_10.11_spmd.sunk | while | flops 2416312320 | bytes 21233992 | solution.py:103
  479.4 5.5 fusion.98
  490.7 5.5 fusion.98
  502.1 5.4 fusion.98
  513.3 5.4 fusion.98
  524.6 5.4 fusion.98
  547.1 5.5 fusion.98
  558.4 5.5 fusion.98
  569.4 6.7 copy.86
  576.1 27.3 %collective-permute-done = bf16[4,192,1024]{2,1,0:T(8,128)(2,1)} collective-permute-done((bf16[4,192,1024]{2,1,0:T(8,128)(2,1)}, bf16[4,192,1024]{2,1,0:T(8,128)(2,1)}, u32[]{:S(2)}, u32[]{:S(2)}) %collective-permute-start) | collective-permute-done | bytes 1572896 | tf_op jit(solution)/shard_map/ppermute | solution.py:11
  603.3 13.0 %fusion.49 = bf16[4,192,4,768]{3,1,2,0:T(8,128)(2,1)S(1)} fusion(bf16[1024,4,768]{2,0,1:T(8,128)(2,1)} %collective-permute-done.1, bf16[1024,4,768]{2,0,1:T(8,128)(2,1)S(1)} %bitcast.171, bf16[4,192,1024]{2,1,0:T(8,128)(2,1)} %collective-permute-done, bf16[4,192,1024]{2,1,0:T(8,128)(2,1)} %multiply_convert_fusion), kind=kOutput, calls=%fused_computation.42 | convolution fusion | flops 9697492992 | bytes 20447232 | tf_op jit(solution)/shard_map/csf,ftj->cstj/dot_general | solution.py:113
  623.2 85.0 %reduce-scatter.5.cloned.1.call-done = bf16[192,3072]{1,0:T(8,128)(2,1)} async-done(((bf16[768,3072]{1,0:T(8,128)(2,1)}), bf16[192,3072]{1,0:T(8,128)(2,1)}) %reduce-scatter.5.cloned.1.call-update) | async-done | bytes 1179664 | tf_op jit(solution)/shard_map/reduce_scatter | solution.py:116
  715.7 15.7 %all-to-all-done.2 = bf16[1,192,4,768]{3,1,0,2:T(8,128)(2,1)S(1)} async-done(((bf16[1,192,4,768]{3,1,0,2:T(8,128)(2,1)}), bf16[1,192,4,768]{3,1,0,2:T(8,128)(2,1)S(1)}, u32[]{:S(2)}, u32[]{:S(2)}) %all-to-all-start.2) | async-done | bytes 1179680 | tf_op jit(solution)/shard_map/all_to_all | solution.py:123
  (76 shorter events, 102.5 us)
Async XLA Ops:
  6.5 180.2 %all-gather.2.cloned.1.call-start = ((), (), s32[]{:S(2)}) async-start(), calls=%async_computation.5 | async-start | bytes 11796480 | tf_op jit(solution)/shard_map/all_gather | solution.py:54
  7.3 214.3 %reduce-scatter.3.cloned.1.call-start = ((), (), s32[]{:S(2)}) async-start(), calls=%async_computation.6 | async-start | bytes 1966080 | tf_op jit(solution)/shard_map/reduce_scatter | solution.py:56
  186.8 7.6 %copy-start.4 = (bf16[768]{0:T(1024)(128)(2,1)S(1)}, bf16[768]{0:T(1024)(128)(2,1)}, u32[]{:S(2)}) copy-start(bf16[768]{0:T(1024)(128)(2,1)} %param.18) | copy-start | bytes 4612
  186.8 7.6 %copy-start.2 = (s32[256,2]{0,1:T(2,128)S(1)}, s32[256,2]{0,1:T(2,128)}, u32[]{:S(2)}) copy-start(s32[256,2]{0,1:T(2,128)} %param.22) | copy-start | bytes 6148
  186.8 34.8 %copy-start = (bf16[256,768]{1,0:T(8,128)(2,1)S(1)}, bf16[256,768]{1,0:T(8,128)(2,1)}, u32[]{:S(2)}) copy-start(bf16[256,768]{1,0:T(8,128)(2,1)} %param.13) | copy-start | bytes 1179652
  260.6 210.5 %all-to-all-start.1 = ((bf16[8,1,4,192,768]{4,3,2,1,0:T(8,128)(2,1)}), bf16[8,1,4,192,768]{4,3,2,1,0:T(8,128)(2,1)}, u32[]{:S(2)}, u32[]{:S(2)}) async-start(bf16[8,1,4,192,768]{4,3,2,1,0:T(8,128)(2,1)} %stack.5), calls=%async_computation.2 | async-start | bytes 18874368 | tf_op jit(solution)/shard_map/all_to_all | solution.py:81
  265.6 442.6 %reduce-scatter.5.cloned.1.call-start = ((), (), s32[]{:S(2)}) async-start(), calls=%async_computation.7 | async-start | bytes 5898240 | tf_op jit(solution)/shard_map/reduce_scatter | solution.py:116
  331.7 244.3 %collective-permute-start.1 = (bf16[1024,4,768]{2,0,1:T(8,128)(2,1)}, bf16[1024,4,768]{2,0,1:T(8,128)(2,1)}, u32[]{:S(2)}, u32[]{:S(2)}) collective-permute-start(bf16[1024,4,768]{2,0,1:T(8,128)(2,1)} %bitcast.145), channel_id=1, source_target_pairs={{0,1},{1,0},{2,3},{3,2},{4,5},{5,4},{6,7},{7,6},{8,9},{9,8},{10,11... | collective-permute-start | bytes 18874376 | tf_op jit(solution)/shard_map/ppermute | solution.py:11
  567.9 35.4 %collective-permute-start = (bf16[4,192,1024]{2,1,0:T(8,128)(2,1)}, bf16[4,192,1024]{2,1,0:T(8,128)(2,1)}, u32[]{:S(2)}, u32[]{:S(2)}) collective-permute-start(bf16[4,192,1024]{2,1,0:T(8,128)(2,1)} %multiply_convert_fusion), channel_id=1, source_target_pairs={{0,1},{1,0},{2,3},{3,2},{4,5},{5,4},{6,7},{7,6},{8,9},{9,8},{10,11... | collective-permute-start | bytes 4718600 | tf_op jit(solution)/shard_map/ppermute | solution.py:11
  623.2 92.4 %copy-start.3 = (s32[256,2]{0,1:T(2,128)S(1)}, s32[256,2]{0,1:T(2,128)}, u32[]{:S(2)}) copy-start(s32[256,2]{0,1:T(2,128)} %param.23) | copy-start | bytes 6148
  623.2 108.2 %copy-start.1 = (bf16[256,768]{1,0:T(8,128)(2,1)S(1)}, bf16[256,768]{1,0:T(8,128)(2,1)}, u32[]{:S(2)}) copy-start(bf16[256,768]{1,0:T(8,128)(2,1)} %reduce-scatter.3.cloned.1.call-done) | copy-start | bytes 1179652
  712.1 19.3 %all-to-all-start.2 = ((bf16[1,192,4,768]{3,1,0,2:T(8,128)(2,1)}), bf16[1,192,4,768]{3,1,0,2:T(8,128)(2,1)S(1)}, u32[]{:S(2)}, u32[]{:S(2)}) async-start(bf16[1,192,4,768]{3,1,0,2:T(8,128)(2,1)} %copy.68), calls=%async_computation.4 | async-start | bytes 2359296 | tf_op jit(solution)/shard_map/all_to_all | solution.py:123
Sparse Core Ops, SparseCore 0:
  8.9 177.8 all-gather.1
  194.4 27.0 reduce-scatter.2
  623.4 84.8 reduce-scatter.4
